TPU v7x, 32 devices: a whole 2x2x4 slice. The times are simulated.
32 devices in a mesh: row: 4 (over x, core), col: 8 (over z, y).
Axes of the slice: x: 2, y: 2, z: 4, core: 2. Of those that a mesh axis runs over, the one named last changes fastest.
Arguments:
- basis_raw: float32 [37, 192, 1024], P(None, 'row', 'col'), may hold values from -4 to 4
- krylov_raw: float32 [4, 37, 34], replicated, may hold values from -6 to 6
- stiffness: float32 [192, 1024], P('row', 'col'), may hold values from -0.4 to 0.4
- rotation: float32 [192, 1024], P('row', 'col'), may hold values from -0.2 to 0.2
Outputs:
- new_columns: float32 [3, 192, 1024], P(None, 'row', 'col')
- coefficients: float32 [4, 40, 37], replicated
- hessenberg: float32 [3, 37], replicated
- gram: float32 [5, 40, 5, 40], replicated
- new_images: float32 [3, 192, 1024], P(None, 'row', 'col')
All inputs are finite; a program needn't handle non-finite values.
Results may differ from a plain program's by a relative error of at most 0.001.
Values sent between devices are 32-bit elements; how exact they have to be, the bound alone decides.
No kernel may reach another device: no remote copies, remote signals or barrier semaphores. Data moves between devices by JAX's collectives and lax.ppermute only.
A program may use at most 64 MiB of HBM per device.

v0:
```python
import jax
import jax.numpy as jnp
from jax import lax
from jax.sharding import PartitionSpec as P

K = 40
STEPS = 3
R = 37
KRYLOV = 34
COUPLING = 0.2
EPSILON = 1e-06
GRAM_SHIFT = 0.05
HIGHEST = lax.Precision.HIGHEST


def padded(x, sides, width):
    for axis, dim in sides:
        peers, length = (lax.axis_size(axis), x.shape[dim])
        up = [(i, (i + 1) % peers) for i in range(peers - 1)]
        down = [(j, i) for i, j in up]
        last = lax.slice_in_dim(x, length - width, length, axis=dim)
        initial = lax.slice_in_dim(x, 0, width, axis=dim)
        before = lax.ppermute(last, axis, up)
        after = lax.ppermute(initial, axis, down)
        x = jnp.concatenate([before, x, after], axis=dim)
    return x


def apply_core(border, diagonal, spin_field):
    middle = border[..., 1:-1, 1:-1]
    left_cells = border[..., 1:-1, :-2]
    right_cells = border[..., 1:-1, 2:]
    upper_cells = border[..., :-2, 1:-1]
    lower_cells = border[..., 2:, 1:-1]
    return (
        diagonal * middle
        - COUPLING * (upper_cells + lower_cells + left_cells + right_cells)
        + spin_field * (right_cells - left_cells)
    )


def lower_inverse(matrix):
    factor = jnp.linalg.cholesky(matrix)
    identity = jnp.eye(matrix.shape[0], dtype=matrix.dtype)
    return lax.linalg.triangular_solve(factor, identity, left_side=True, lower=True)


def trimmed(source, margin):
    if margin == 0:
        return source
    return source[..., margin:-margin, margin:-margin]


def inside_mask(margin, row_count, col_count):
    row_first = lax.axis_index("row") * row_count - margin
    col_first = lax.axis_index("col") * col_count - margin
    row_global = row_first + lax.iota(jnp.int32, row_count + 2 * margin)
    col_global = col_first + lax.iota(jnp.int32, col_count + 2 * margin)
    row_valid = (row_global >= 0) & (row_global < row_count * lax.axis_size("row"))
    col_valid = (col_global >= 0) & (col_global < col_count * lax.axis_size("col"))
    return (row_valid[:, None] & col_valid[None, :]).astype(jnp.float32)


def local(basis_raw, krylov_raw, stiffness, rotation):
    row_count = basis_raw.shape[1]
    col_count = basis_raw.shape[2]
    cell_count = row_count * col_count
    grid_total = cell_count * lax.axis_size("row") * lax.axis_size("col")
    inverse_total = 1.0 / grid_total
    flat_raw = basis_raw.reshape(R, cell_count)
    raw_gram = (
        lax.psum(jnp.dot(flat_raw, flat_raw.T, precision=HIGHEST), ("row", "col")) * inverse_total
    )
    inverse_factor = lower_inverse(raw_gram + GRAM_SHIFT * jnp.eye(R, dtype=jnp.float32))
    prepared = jnp.dot(inverse_factor, flat_raw, precision=HIGHEST)
    basis_rows = jnp.concatenate([prepared, jnp.zeros((STEPS, cell_count), jnp.float32)], 0)
    krylov_flat = krylov_raw.reshape(4 * R, KRYLOV)
    krylov_ortho = jnp.dot(
        krylov_flat,
        lower_inverse(jnp.dot(krylov_flat.T, krylov_flat, precision=HIGHEST)).T,
        precision=HIGHEST,
    )
    krylov_width = KRYLOV + STEPS
    krylov_rows = jnp.pad(krylov_ortho.reshape(4, R, KRYLOV), ((0, 0), (0, STEPS), (0, STEPS)))
    field_rim = padded(jnp.stack([stiffness, rotation]), (("row", 1), ("col", 2)), 3)

    def shrink(extended, margin):
        diagonal = trimmed(field_rim[0], 4 - margin)
        spin_field = trimmed(field_rim[1], 4 - margin)
        return apply_core(extended, diagonal, spin_field) * inside_mask(
            margin - 1, row_count, col_count
        )

    hessen_rows = []
    for turn_index in range(STEPS):
        column = KRYLOV + turn_index
        new_row = R + turn_index
        latest = krylov_rows[:, :, column - 1]
        components = jnp.dot(latest, basis_rows, precision=HIGHEST).reshape(4, row_count, col_count)
        block_rim = padded(components, (("row", 1), ("col", 2)), 4)
        section_four = block_rim[3]
        section_three = trimmed(block_rim[2], 1) + 2.0 * shrink(section_four, 4)
        section_two = (
            trimmed(block_rim[1], 2) + 2.0 * shrink(section_three, 3) - trimmed(section_four, 2)
        )
        section_one = (
            trimmed(block_rim[0], 3) + 2.0 * shrink(section_two, 2) - trimmed(section_three, 2)
        )
        summed = shrink(section_one, 1) - trimmed(section_two, 2)
        target = (0.5 * components[2] - 0.5 * summed).reshape(cell_count)
        first_coef = (
            lax.psum(jnp.dot(basis_rows, target, precision=HIGHEST), ("row", "col")) * inverse_total
        )
        residual_one = target - jnp.dot(first_coef, basis_rows, precision=HIGHEST)
        second_coef = (
            lax.psum(jnp.dot(basis_rows, residual_one, precision=HIGHEST), ("row", "col"))
            * inverse_total
        )
        residual_two = residual_one - jnp.dot(second_coef, basis_rows, precision=HIGHEST)
        square = lax.psum(jnp.sum(residual_two * residual_two), ("row", "col")) * inverse_total
        new_norm = jnp.sqrt(square + EPSILON)
        basis_rows = basis_rows.at[new_row].set(residual_two / new_norm)
        unit_row = (jnp.arange(K) == new_row).astype(jnp.float32)
        expanded = jnp.stack(
            [
                latest[1],
                0.5 * (latest[0] + latest[2]),
                0.5 * (latest[1] + latest[3]),
                first_coef + second_coef + new_norm * unit_row,
            ]
        ).reshape(4 * K)
        matrix_view = krylov_rows.reshape(4 * K, krylov_width)
        first_proj = jnp.dot(expanded, matrix_view, precision=HIGHEST)
        ortho_one = expanded - jnp.dot(matrix_view, first_proj, precision=HIGHEST)
        second_proj = jnp.dot(ortho_one, matrix_view, precision=HIGHEST)
        ortho_two = ortho_one - jnp.dot(matrix_view, second_proj, precision=HIGHEST)
        krylov_norm = jnp.sqrt(jnp.sum(ortho_two * ortho_two) + EPSILON)
        krylov_rows = krylov_rows.at[:, :, column].set((ortho_two / krylov_norm).reshape(4, K))
        unit_column = (jnp.arange(krylov_width) == column).astype(jnp.float32)
        hessen_rows.append(first_proj + second_proj + krylov_norm * unit_column)
    new_columns = basis_rows[R:].reshape(STEPS, row_count, col_count)
    order_zero = padded(basis_rows.reshape(K, row_count, col_count), (("row", 1), ("col", 2)), 4)
    order_one = shrink(order_zero, 4)
    order_two = 2.0 * shrink(order_one, 3) - trimmed(order_zero, 2)
    order_three = 2.0 * shrink(order_two, 2) - trimmed(order_one, 2)
    order_four = 2.0 * shrink(order_three, 1) - trimmed(order_two, 2)
    polynomials = [
        trimmed(order_zero, 4),
        trimmed(order_one, 3),
        trimmed(order_two, 2),
        trimmed(order_three, 1),
        order_four,
    ]
    new_images = polynomials[4][R:]
    band_rows = row_count // 8

    def accumulate(band_index, gram_sum):
        band_start = band_index * band_rows
        band_tile = jnp.concatenate(
            [
                lax.dynamic_slice_in_dim(poly_field, band_start, band_rows, 1).reshape(
                    K, band_rows * col_count
                )
                for poly_field in polynomials
            ],
            0,
        )
        return gram_sum + jnp.dot(band_tile, band_tile.T, precision=HIGHEST)

    local_gram = lax.fori_loop(0, 8, accumulate, jnp.zeros((5 * K, 5 * K), jnp.float32))
    gram = (lax.psum(local_gram, ("row", "col")) * inverse_total).reshape(5, K, 5, K)
    return (new_columns, krylov_rows, jnp.stack(hessen_rows), gram, new_images)


def solution(mesh):
    in_specs = (P(None, "row", "col"), P(), P("row", "col"), P("row", "col"))
    out_specs = (P(None, "row", "col"), P(), P(), P(), P(None, "row", "col"))
    return jax.shard_map(local, mesh=mesh, in_specs=in_specs, out_specs=out_specs, check_vma=False)
```

profile of v0, /device:TPU:8, one launch (start us, length us, event | category | flops | bytes accessed | tf_op | source)
XLA Modules:
  0.0 758.2 jit_solution(2868353420702078962)
XLA Ops:
  23.4 43.2 %psum.77 = f32[37,37]{1,0:T(8,128)S(1)} all-reduce(f32[37,37]{1,0:T(8,128)S(1)} %convolution_bitcast_fusion.2), channel_id=1, replica_groups=mesh['row'=4,'col'=8] {'row','col'}, use_global_device_ids=true, to_apply=%region_0.0 | all-reduce | flops 1369 | bytes 10952 | tf_op jit(solution)/shard_map/psum | solution.py:72
  81.1 4.2 collective-permute-start.2
  95.1 3.4 collective-permute-start.7
  105.5 42.1 %psum.78 = f32[40]{0:T(128)S(1)} all-reduce(f32[40]{0:T(128)S(1)} %convolution_bitcast_fusion.8), channel_id=1, replica_groups=mesh['row'=4,'col'=8] {'row','col'}, use_global_device_ids=true, to_apply=%region_5.6 | all-reduce | flops 40 | bytes 320 | tf_op jit(solution)/shard_map/psum | solution.py:112
  149.1 40.9 %psum.79 = f32[40]{0:T(128)S(1)} all-reduce(f32[40]{0:T(128)S(1)} %convolution_bitcast_fusion.7), channel_id=1, replica_groups=mesh['row'=4,'col'=8] {'row','col'}, use_global_device_ids=true, to_apply=%region_6.7 | all-reduce | flops 40 | bytes 320 | tf_op jit(solution)/shard_map/psum | solution.py:116
  191.3 39.6 %psum.80 = f32[]{:T(128)} all-reduce(f32[]{:T(128)} %get-tuple-element.284), channel_id=1, replica_groups=mesh['row'=4,'col'=8] {'row','col'}, use_global_device_ids=true, to_apply=%region_8.9 | all-reduce | flops 1 | bytes 8 | tf_op jit(solution)/shard_map/psum | solution.py:120
  238.3 3.7 collective-permute-done.9
  245.3 3.5 collective-permute-start.11
  254.6 40.2 %psum.81 = f32[40]{0:T(128)S(1)} all-reduce(f32[40]{0:T(128)S(1)} %convolution_bitcast_fusion.6), channel_id=1, replica_groups=mesh['row'=4,'col'=8] {'row','col'}, use_global_device_ids=true, to_apply=%region_10.11 | all-reduce | flops 40 | bytes 320 | tf_op jit(solution)/shard_map/psum | solution.py:112
  296.3 39.7 %psum.82 = f32[40]{0:T(128)S(1)} all-reduce(f32[40]{0:T(128)S(1)} %convolution_bitcast_fusion.5), channel_id=1, replica_groups=mesh['row'=4,'col'=8] {'row','col'}, use_global_device_ids=true, to_apply=%region_11.12 | all-reduce | flops 40 | bytes 320 | tf_op jit(solution)/shard_map/psum | solution.py:116
  337.2 40.3 %psum.83 = f32[]{:T(128)} all-reduce(f32[]{:T(128)} %get-tuple-element.280), channel_id=1, replica_groups=mesh['row'=4,'col'=8] {'row','col'}, use_global_device_ids=true, to_apply=%region_13.14 | all-reduce | flops 1 | bytes 8 | tf_op jit(solution)/shard_map/psum | solution.py:120
  384.4 4.1 collective-permute-done.13
  391.2 4.2 collective-permute-start.15
  396.2 3.7 collective-permute-done.15
  401.7 39.8 %psum.84 = f32[40]{0:T(128)S(1)} all-reduce(f32[40]{0:T(128)S(1)} %convolution_bitcast_fusion.4), channel_id=1, replica_groups=mesh['row'=4,'col'=8] {'row','col'}, use_global_device_ids=true, to_apply=%region_15.16 | all-reduce | flops 40 | bytes 320 | tf_op jit(solution)/shard_map/psum | solution.py:112
  442.9 38.8 %psum.85 = f32[40]{0:T(128)S(1)} all-reduce(f32[40]{0:T(128)S(1)} %convolution_bitcast_fusion.3), channel_id=1, replica_groups=mesh['row'=4,'col'=8] {'row','col'}, use_global_device_ids=true, to_apply=%region_16.17 | all-reduce | flops 40 | bytes 320 | tf_op jit(solution)/shard_map/psum | solution.py:116
  483.0 41.2 %psum.86 = f32[]{:T(128)} all-reduce(f32[]{:T(128)} %get-tuple-element.276), channel_id=1, replica_groups=mesh['row'=4,'col'=8] {'row','col'}, use_global_device_ids=true, to_apply=%region_18.19 | all-reduce | flops 1 | bytes 8 | tf_op jit(solution)/shard_map/psum | solution.py:120
  530.5 3.7 collective-permute-start.16
  544.2 4.5 collective-permute-start.18
  565.2 5.1 slice_subtract_fusion
  570.4 3.7 slice_subtract_fusion.1
  574.1 5.1 fusion.27
  587.4 33.6 %while.20 = (s32[]{:T(128)}, f32[200,200]{1,0:T(8,128)S(1)}, f32[40,48,128]{2,1,0:T(8,128)}, f32[40,48,128]{2,1,0:T(8,128)}, f32[40,48,128]{2,1,0:T(8,128)}, /*i...) while((s32[]{:T(128)}, f32[200,200]{1,0:T(8,128)S(1)}, ...), condition=%wide.region_21.22_spmd.clone, body=%wide.region_20.21_spmd.clone.sunk | while | flops 368720000 | bytes 3556025 | solution.py:170
  623.1 126.0 %all-reduce.4.cloned.1.call-done = f32[200,200]{1,0:T(8,128)} async-done(((f32[200,200]{1,0:T(8,128)}), f32[200,200]{1,0:T(8,128)}) %all-reduce.4.cloned.1.call-update) | async-done | bytes 160016 | tf_op jit(solution)/shard_map/psum | solution.py:171
  (342 shorter events, 157.2 us)
Async XLA Ops:
  7.2 741.9 %all-reduce.4.cloned.1.call-start = ((), (), s32[]{:S(2)}) async-start(), calls=%async_computation | async-start | bytes 409600 | tf_op jit(solution)/shard_map/psum | solution.py:171
  8.0 73.1 %collective-permute-start = (f32[2,3,128]{2,1,0:T(4,128)S(1)}, f32[2,3,128]{2,1,0:T(4,128)S(1)}, u32[]{:S(2)}, u32[]{:S(2)}) collective-permute-start(f32[2,3,128]{2,1,0:T(4,128)S(1)} %get-tuple-element.336), channel_id=1, source_target_pairs={{0,8},{8,16},{16,24},{1,9},{9,17},{17,25},{2,10},{10,18},{18,26},{... | collective-permute-start | bytes 9224 | tf_op jit(solution)/shard_map/ppermute | solution.py:23
  9.7 71.3 %collective-permute-start.1 = (f32[2,3,128]{2,1,0:T(4,128)S(1)}, f32[2,3,128]{2,1,0:T(4,128)S(1)}, u32[]{:S(2)}, u32[]{:S(2)}) collective-permute-start(f32[2,3,128]{2,1,0:T(4,128)S(1)} %get-tuple-element.337), channel_id=1, source_target_pairs={{8,0},{16,8},{24,16},{9,1},{17,9},{25,17},{10,2},{18,10},{26,18},{... | collective-permute-start | bytes 9224 | tf_op jit(solution)/shard_map/ppermute | solution.py:24
  77.9 13.7 %collective-permute-start.4 = (f32[4,4,128]{2,1,0:T(4,128)S(1)}, f32[4,4,128]{2,1,0:T(4,128)S(1)}, u32[]{:S(2)}, u32[]{:S(2)}) collective-permute-start(f32[4,4,128]{2,1,0:T(4,128)S(1)} %get-tuple-element.321), channel_id=1, source_target_pairs={{0,8},{8,16},{16,24},{1,9},{9,17},{17,25},{2,10},{10,18},{18,26},{... | collective-permute-start | bytes 24584 | tf_op jit(solution)/shard_map/ppermute | solution.py:23
  79.2 12.4 %collective-permute-start.5 = (f32[4,4,128]{2,1,0:T(4,128)S(1)}, f32[4,4,128]{2,1,0:T(4,128)S(1)}, u32[]{:S(2)}, u32[]{:S(2)}) collective-permute-start(f32[4,4,128]{2,1,0:T(4,128)S(1)} %get-tuple-element.322), channel_id=1, source_target_pairs={{8,0},{16,8},{24,16},{9,1},{17,9},{25,17},{10,2},{18,10},{26,18},{... | collective-permute-start | bytes 24584 | tf_op jit(solution)/shard_map/ppermute | solution.py:24
  81.1 8.5 %collective-permute-start.2 = (f32[2,54,3]{2,1,0:T(8,128)S(1)}, f32[2,54,3]{2,1,0:T(8,128)S(1)}, u32[]{:S(2)}, u32[]{:S(2)}) collective-permute-start(f32[2,54,3]{2,1,0:T(8,128)S(1)} %get-tuple-element.334), channel_id=1, source_target_pairs={{0,1},{1,2},{2,3},{3,4},{4,5},{5,6},{6,7},{8,9},{9,10},{10,11},{11... | collective-permute-start | bytes 3896 | tf_op jit(solution)/shard_map/ppermute | solution.py:23
  85.4 6.1 collective-permute-start.3
  91.7 8.5 %collective-permute-start.6 = (f32[4,56,4]{2,1,0:T(8,128)S(1)}, f32[4,56,4]{2,1,0:T(8,128)S(1)}, u32[]{:S(2)}, u32[]{:S(2)}) collective-permute-start(f32[4,56,4]{2,1,0:T(8,128)S(1)} %get-tuple-element.315), channel_id=1, source_target_pairs={{0,1},{1,2},{2,3},{3,4},{4,5},{5,6},{6,7},{8,9},{9,10},{10,11},{11... | collective-permute-start | bytes 10760 | tf_op jit(solution)/shard_map/ppermute | solution.py:23
  95.1 7.1 collective-permute-start.7
  103.7 127.9 %copy-start.23 = (f32[1,40]{1,0:T(1,128)S(1)}, f32[1,40]{1,0:T(1,128)}, u32[]{:S(2)}) copy-start(f32[1,40]{1,0:T(1,128)} %fusion.166) | copy-start | bytes 484
  148.2 103.0 %copy-start.14 = (f32[48,128]{1,0:T(8,128)S(1)}, f32[48,128]{1,0:T(8,128)}, u32[]{:S(2)}) copy-start(f32[48,128]{1,0:T(8,128)} %get-tuple-element.327) | copy-start | bytes 73732
  190.6 62.6 %copy-start.16 = (pred[52]{0:T(512)(128)(4,1)S(1)}, pred[52]{0:T(512)(128)(4,1)}, u32[]{:S(2)}) copy-start(pred[52]{0:T(512)(128)(4,1)} %copy-done.15) | copy-start | bytes 160
  235.1 3.2 collective-permute-start.8
  236.4 5.6 collective-permute-start.9
  242.1 10.7 %collective-permute-start.10 = (f32[4,56,4]{2,1,0:T(8,128)S(1)}, f32[4,56,4]{2,1,0:T(8,128)S(1)}, u32[]{:S(2)}, u32[]{:S(2)}) collective-permute-start(f32[4,56,4]{2,1,0:T(8,128)S(1)} %get-tuple-element.311), channel_id=1, source_target_pairs={{0,1},{1,2},{2,3},{3,4},{4,5},{5,6},{6,7},{8,9},{9,10},{10,11},{11... | collective-permute-start | bytes 10760 | tf_op jit(solution)/shard_map/ppermute | solution.py:23
  245.3 7.5 collective-permute-start.11
  381.6 2.8 collective-permute-start.12
  382.9 5.6 collective-permute-start.13
  388.6 7.6 %collective-permute-start.14 = (f32[4,56,4]{2,1,0:T(8,128)S(1)}, f32[4,56,4]{2,1,0:T(8,128)S(1)}, u32[]{:S(2)}, u32[]{:S(2)}) collective-permute-start(f32[4,56,4]{2,1,0:T(8,128)S(1)} %get-tuple-element.309), channel_id=1, source_target_pairs={{0,1},{1,2},{2,3},{3,4},{4,5},{5,6},{6,7},{8,9},{9,10},{10,11},{11... | collective-permute-start | bytes 10760 | tf_op jit(solution)/shard_map/ppermute | solution.py:23
  391.2 8.7 %collective-permute-start.15 = (f32[4,56,4]{2,1,0:T(8,128)S(1)}, f32[4,56,4]{2,1,0:T(8,128)S(1)}, u32[]{:S(2)}, u32[]{:S(2)}) collective-permute-start(f32[4,56,4]{2,1,0:T(8,128)S(1)} %get-tuple-element.310), channel_id=1, source_target_pairs={{1,0},{2,1},{3,2},{4,3},{5,4},{6,5},{7,6},{9,8},{10,9},{11,10},{12... | collective-permute-start | bytes 10760 | tf_op jit(solution)/shard_map/ppermute | solution.py:24
  529.2 10.4 %collective-permute-start.17 = (f32[40,4,128]{2,0,1:T(8,128)}, f32[40,4,128]{2,0,1:T(8,128)}, u32[]{:S(2)}, u32[]{:S(2)}) collective-permute-start(f32[40,4,128]{2,0,1:T(8,128)} %copy.100), channel_id=1, source_target_pairs={{8,0},{16,8},{24,16},{9,1},{17,9},{25,17},{10,2},{18,10},{26,18},{... | collective-permute-start | bytes 245768 | tf_op jit(solution)/shard_map/ppermute | solution.py:24
  530.5 6.0 collective-permute-start.16
  544.2 7.9 %collective-permute-start.18 = (f32[40,56,4]{1,0,2:T(8,128)S(1)}, f32[40,56,4]{1,0,2:T(8,128)S(1)}, u32[]{:S(2)}, u32[]{:S(2)}) collective-permute-start(f32[40,56,4]{1,0,2:T(8,128)S(1)} %get-tuple-element.290), channel_id=1, source_target_pairs={{0,1},{1,2},{2,3},{3,4},{4,5},{5,6},{6,7},{8,9},{9,10},{10,11},{11... | collective-permute-start | bytes 107528 | tf_op jit(solution)/shard_map/ppermute | solution.py:23
  548.7 6.3 collective-permute-start.19
  (22 other events, 381.2 us)
Sparse Core Ops, SparseCore 0:
  621.8 127.2 all-reduce.3
where the time goes:
time: 768 us; the launch traced here: 758 us
  blocking collectives  406 us (53%)
  waiting for transfers between devices  146 us (19%)
  local copies, waits for them, and re-layouts  65.8 us (9%)
  starting transfers between devices  49.6 us (6%)
  other arithmetic  46.6 us (6%)
  matrix products  24 us (3%)
  between operations  19.7 us (3%)
    psum x1, waiting for transfers between devices, local(): lax.psum(local_gram, ('row', 'col')) * inverse_total  126 us
    psum x3, blocking collectives, local(): lax.psum(jnp.dot(basis_rows, target, precision=HIGHEST), ('row', 'col'))  122 us
    psum x3, blocking collectives, local(): lax.psum(jnp.sum(residual_two * residual_two), ('row', 'col'))  121 us
    psum x3, blocking collectives, local(): lax.psum(jnp.dot(basis_rows, residual_one, precision=HIGHEST), ('row', 'c...  119 us
    psum x1, blocking collectives, local(): lax.psum(jnp.dot(flat_raw, flat_raw.T, precision=HIGHEST), ('row', 'col'))  43.2 us
    ppermute x10, starting transfers between devices, padded(): before = lax.ppermute(last, axis, up)  27.1 us
    dynamic_slice x24, local copies, waits for them, and re-layouts, accumulate(): lax.dynamic_slice_in_dim(poly_field, band_start, band_rows, 1)  25.9 us
    ppermute x10, starting transfers between devices, padded(): after = lax.ppermute(initial, axis, down)  22.4 us
  transfers between devices with their start and end apart: 21, of which 10 were waited for; matrix products, arithmetic and copies ran while one was open for 5% of the time, Pallas kernels for 0%

commit v1 on v0

--- a/solution.py
+++ b/solution.py
@@ -109,7 +109,8 @@
         summed = shrink(section_one, 1) - trimmed(section_two, 2)
         target = (0.5 * components[2] - 0.5 * summed).reshape(cell_count)
         first_coef = (
-            lax.psum(jnp.dot(basis_rows, target, precision=HIGHEST), ("row", "col")) * inverse_total
+            lax.psum(lax.psum(jnp.dot(basis_rows, target, precision=HIGHEST), "col"), "row")
+            * inverse_total
         )
         residual_one = target - jnp.dot(first_coef, basis_rows, precision=HIGHEST)
         second_coef = (

time: 768 us -> 718 us (0.935)
  blocking collectives: 406 us -> 355 us
    psum x3 -> x6, blocking collectives: 122 us -> 69.1 us  [the longest x3 51.2 us: local(): lax.psum(jnp.dot(basis_rows, target, precision=HIGHEST), 'col')]
where the time goes in v1:
time: 718 us; the launch traced here: 709 us
  blocking collectives  355 us (49%)
  waiting for transfers between devices  146 us (20%)
  local copies, waits for them, and re-layouts  65.7 us (9%)
  starting transfers between devices  50.7 us (7%)
  other arithmetic  46.7 us (7%)
  matrix products  24 us (3%)
  between operations  19.7 us (3%)
    psum x1, waiting for transfers between devices, local(): lax.psum(local_gram, ('row', 'col')) * inverse_total  126 us
    psum x3, blocking collectives, local(): lax.psum(jnp.dot(basis_rows, residual_one, precision=HIGHEST), ('row', 'c...  125 us
    psum x3, blocking collectives, local(): lax.psum(jnp.sum(residual_two * residual_two), ('row', 'col'))  118 us
    psum x3, blocking collectives, local(): lax.psum(jnp.dot(basis_rows, target, precision=HIGHEST), 'col')  51.2 us
    psum x1, blocking collectives, local(): lax.psum(jnp.dot(flat_raw, flat_raw.T, precision=HIGHEST), ('row', 'col'))  43.2 us
    ppermute x10, starting transfers between devices, padded(): before = lax.ppermute(last, axis, up)  26.9 us
    dynamic_slice x24, local copies, waits for them, and re-layouts, accumulate(): lax.dynamic_slice_in_dim(poly_field, band_start, band_rows, 1)  25.9 us
    ppermute x10, starting transfers between devices, padded(): after = lax.ppermute(initial, axis, down)  23.7 us
  transfers between devices with their start and end apart: 21, of which 10 were waited for; matrix products, arithmetic and copies ran while one was open for 5% of the time, Pallas kernels for 0%

profile of v1, /device:TPU:8, one launch (start us, length us, event | category | flops | bytes accessed | tf_op | source)
XLA Modules:
  0.0 708.5 jit_solution(10748870942867191914)
XLA Ops:
  23.4 43.2 %psum.98 = f32[37,37]{1,0:T(8,128)S(1)} all-reduce(f32[37,37]{1,0:T(8,128)S(1)} %convolution_bitcast_fusion.2), channel_id=1, replica_groups=mesh['row'=4,'col'=8] {'row','col'}, use_global_device_ids=true, to_apply=%region_0.0 | all-reduce | flops 1369 | bytes 10952 | tf_op jit(solution)/shard_map/psum | solution.py:72
  81.1 4.2 collective-permute-start.2
  105.5 17.7 %psum.99 = f32[40]{0:T(128)S(1)} all-reduce(f32[40]{0:T(128)S(1)} %convolution_bitcast_fusion.8), channel_id=1, replica_groups=mesh['row'=4,'col'=8] {'col'}, use_global_device_ids=true, to_apply=%region_5.6 | all-reduce | flops 40 | bytes 320 | tf_op jit(solution)/shard_map/psum | solution.py:112
  123.2 6.3 psum.100
  130.9 42.7 %psum.101 = f32[40]{0:T(128)S(1)} all-reduce(f32[40]{0:T(128)S(1)} %convolution_bitcast_fusion.7), channel_id=1, replica_groups=mesh['row'=4,'col'=8] {'row','col'}, use_global_device_ids=true, to_apply=%region_7.8 | all-reduce | flops 40 | bytes 320 | tf_op jit(solution)/shard_map/psum | solution.py:117
  174.9 38.9 %psum.102 = f32[]{:T(128)} all-reduce(f32[]{:T(128)} %get-tuple-element.284), channel_id=1, replica_groups=mesh['row'=4,'col'=8] {'row','col'}, use_global_device_ids=true, to_apply=%region_9.10 | all-reduce | flops 1 | bytes 8 | tf_op jit(solution)/shard_map/psum | solution.py:121
  237.9 17.1 %psum.103 = f32[40]{0:T(128)S(1)} all-reduce(f32[40]{0:T(128)S(1)} %convolution_bitcast_fusion.6), channel_id=1, replica_groups=mesh['row'=4,'col'=8] {'col'}, use_global_device_ids=true, to_apply=%region_11.12 | all-reduce | flops 40 | bytes 320 | tf_op jit(solution)/shard_map/psum | solution.py:112
  254.9 5.8 psum.104
  262.2 41.2 %psum.105 = f32[40]{0:T(128)S(1)} all-reduce(f32[40]{0:T(128)S(1)} %convolution_bitcast_fusion.5), channel_id=1, replica_groups=mesh['row'=4,'col'=8] {'row','col'}, use_global_device_ids=true, to_apply=%region_13.14 | all-reduce | flops 40 | bytes 320 | tf_op jit(solution)/shard_map/psum | solution.py:117
  304.6 40.0 %psum.106 = f32[]{:T(128)} all-reduce(f32[]{:T(128)} %get-tuple-element.280), channel_id=1, replica_groups=mesh['row'=4,'col'=8] {'row','col'}, use_global_device_ids=true, to_apply=%region_15.16 | all-reduce | flops 1 | bytes 8 | tf_op jit(solution)/shard_map/psum | solution.py:121
  351.4 4.1 collective-permute-done.13
  358.0 4.4 collective-permute-start.15
  363.2 3.8 collective-permute-done.15
  368.8 16.5 %psum.107 = f32[40]{0:T(128)S(1)} all-reduce(f32[40]{0:T(128)S(1)} %convolution_bitcast_fusion.4), channel_id=1, replica_groups=mesh['row'=4,'col'=8] {'col'}, use_global_device_ids=true, to_apply=%region_17.18 | all-reduce | flops 40 | bytes 320 | tf_op jit(solution)/shard_map/psum | solution.py:112
  385.2 5.8 psum.108
  392.5 40.9 %psum.109 = f32[40]{0:T(128)S(1)} all-reduce(f32[40]{0:T(128)S(1)} %convolution_bitcast_fusion.3), channel_id=1, replica_groups=mesh['row'=4,'col'=8] {'row','col'}, use_global_device_ids=true, to_apply=%region_19.20 | all-reduce | flops 40 | bytes 320 | tf_op jit(solution)/shard_map/psum | solution.py:117
  434.6 39.4 %psum.110 = f32[]{:T(128)} all-reduce(f32[]{:T(128)} %get-tuple-element.276), channel_id=1, replica_groups=mesh['row'=4,'col'=8] {'row','col'}, use_global_device_ids=true, to_apply=%region_21.22 | all-reduce | flops 1 | bytes 8 | tf_op jit(solution)/shard_map/psum | solution.py:121
  480.3 3.7 collective-permute-start.16
  494.0 4.5 collective-permute-start.18
  515.1 5.1 slice_subtract_fusion
  520.2 3.7 slice_subtract_fusion.1
  524.0 5.2 fusion.27
  537.2 33.6 %while.20 = (s32[]{:T(128)}, f32[200,200]{1,0:T(8,128)S(1)}, f32[40,48,128]{2,1,0:T(8,128)}, f32[40,48,128]{2,1,0:T(8,128)}, f32[40,48,128]{2,1,0:T(8,128)}, /*i...) while((s32[]{:T(128)}, f32[200,200]{1,0:T(8,128)S(1)}, ...), condition=%wide.region_24.25_spmd.clone, body=%wide.region_23.24_spmd.clone.sunk | while | flops 368720000 | bytes 3556025 | solution.py:171
  572.9 126.5 %all-reduce.4.cloned.1.call-done = f32[200,200]{1,0:T(8,128)} async-done(((f32[200,200]{1,0:T(8,128)}), f32[200,200]{1,0:T(8,128)}) %all-reduce.4.cloned.1.call-update) | async-done | bytes 160016 | tf_op jit(solution)/shard_map/psum | solution.py:172
  (345 shorter events, 167.8 us)
Async XLA Ops:
  7.2 692.2 %all-reduce.4.cloned.1.call-start = ((), (), s32[]{:S(2)}) async-start(), calls=%async_computation | async-start | bytes 409600 | tf_op jit(solution)/shard_map/psum | solution.py:172
  8.0 73.1 %collective-permute-start = (f32[2,3,128]{2,1,0:T(4,128)S(1)}, f32[2,3,128]{2,1,0:T(4,128)S(1)}, u32[]{:S(2)}, u32[]{:S(2)}) collective-permute-start(f32[2,3,128]{2,1,0:T(4,128)S(1)} %get-tuple-element.336), channel_id=1, source_target_pairs={{0,8},{8,16},{16,24},{1,9},{9,17},{17,25},{2,10},{10,18},{18,26},{... | collective-permute-start | bytes 9224 | tf_op jit(solution)/shard_map/ppermute | solution.py:23
  9.7 71.3 %collective-permute-start.1 = (f32[2,3,128]{2,1,0:T(4,128)S(1)}, f32[2,3,128]{2,1,0:T(4,128)S(1)}, u32[]{:S(2)}, u32[]{:S(2)}) collective-permute-start(f32[2,3,128]{2,1,0:T(4,128)S(1)} %get-tuple-element.337), channel_id=1, source_target_pairs={{8,0},{16,8},{24,16},{9,1},{17,9},{25,17},{10,2},{18,10},{26,18},{... | collective-permute-start | bytes 9224 | tf_op jit(solution)/shard_map/ppermute | solution.py:24
  77.9 13.7 %collective-permute-start.4 = (f32[4,4,128]{2,1,0:T(4,128)S(1)}, f32[4,4,128]{2,1,0:T(4,128)S(1)}, u32[]{:S(2)}, u32[]{:S(2)}) collective-permute-start(f32[4,4,128]{2,1,0:T(4,128)S(1)} %get-tuple-element.321), channel_id=1, source_target_pairs={{0,8},{8,16},{16,24},{1,9},{9,17},{17,25},{2,10},{10,18},{18,26},{... | collective-permute-start | bytes 24584 | tf_op jit(solution)/shard_map/ppermute | solution.py:23
  79.2 12.4 %collective-permute-start.5 = (f32[4,4,128]{2,1,0:T(4,128)S(1)}, f32[4,4,128]{2,1,0:T(4,128)S(1)}, u32[]{:S(2)}, u32[]{:S(2)}) collective-permute-start(f32[4,4,128]{2,1,0:T(4,128)S(1)} %get-tuple-element.322), channel_id=1, source_target_pairs={{8,0},{16,8},{24,16},{9,1},{17,9},{25,17},{10,2},{18,10},{26,18},{... | collective-permute-start | bytes 24584 | tf_op jit(solution)/shard_map/ppermute | solution.py:24
  81.1 8.5 %collective-permute-start.2 = (f32[2,54,3]{2,1,0:T(8,128)S(1)}, f32[2,54,3]{2,1,0:T(8,128)S(1)}, u32[]{:S(2)}, u32[]{:S(2)}) collective-permute-start(f32[2,54,3]{2,1,0:T(8,128)S(1)} %get-tuple-element.334), channel_id=1, source_target_pairs={{0,1},{1,2},{2,3},{3,4},{4,5},{5,6},{6,7},{8,9},{9,10},{10,11},{11... | collective-permute-start | bytes 3896 | tf_op jit(solution)/shard_map/ppermute | solution.py:23
  85.4 6.1 collective-permute-start.3
  91.7 8.4 %collective-permute-start.6 = (f32[4,56,4]{2,1,0:T(8,128)S(1)}, f32[4,56,4]{2,1,0:T(8,128)S(1)}, u32[]{:S(2)}, u32[]{:S(2)}) collective-permute-start(f32[4,56,4]{2,1,0:T(8,128)S(1)} %get-tuple-element.315), channel_id=1, source_target_pairs={{0,1},{1,2},{2,3},{3,4},{4,5},{5,6},{6,7},{8,9},{9,10},{10,11},{11... | collective-permute-start | bytes 10760 | tf_op jit(solution)/shard_map/ppermute | solution.py:23
  95.1 7.1 collective-permute-start.7
  103.7 110.8 %copy-start.23 = (f32[1,40]{1,0:T(1,128)S(1)}, f32[1,40]{1,0:T(1,128)}, u32[]{:S(2)}) copy-start(f32[1,40]{1,0:T(1,128)} %fusion.166) | copy-start | bytes 484
  130.0 104.1 %copy-start.14 = (f32[48,128]{1,0:T(8,128)S(1)}, f32[48,128]{1,0:T(8,128)}, u32[]{:S(2)}) copy-start(f32[48,128]{1,0:T(8,128)} %get-tuple-element.327) | copy-start | bytes 73732
  174.2 62.2 %copy-start.16 = (pred[52]{0:T(512)(128)(4,1)S(1)}, pred[52]{0:T(512)(128)(4,1)}, u32[]{:S(2)}) copy-start(pred[52]{0:T(512)(128)(4,1)} %copy-done.15) | copy-start | bytes 160
  218.0 3.3 collective-permute-start.8
  219.3 5.6 collective-permute-start.9
  225.0 10.7 %collective-permute-start.10 = (f32[4,56,4]{2,1,0:T(8,128)S(1)}, f32[4,56,4]{2,1,0:T(8,128)S(1)}, u32[]{:S(2)}, u32[]{:S(2)}) collective-permute-start(f32[4,56,4]{2,1,0:T(8,128)S(1)} %get-tuple-element.311), channel_id=1, source_target_pairs={{0,1},{1,2},{2,3},{3,4},{4,5},{5,6},{6,7},{8,9},{9,10},{10,11},{11... | collective-permute-start | bytes 10760 | tf_op jit(solution)/shard_map/ppermute | solution.py:23
  228.2 7.8 %collective-permute-start.11 = (f32[4,56,4]{2,1,0:T(8,128)S(1)}, f32[4,56,4]{2,1,0:T(8,128)S(1)}, u32[]{:S(2)}, u32[]{:S(2)}) collective-permute-start(f32[4,56,4]{2,1,0:T(8,128)S(1)} %get-tuple-element.312), channel_id=1, source_target_pairs={{1,0},{2,1},{3,2},{4,3},{5,4},{6,5},{7,6},{9,8},{10,9},{11,10},{12... | collective-permute-start | bytes 10760 | tf_op jit(solution)/shard_map/ppermute | solution.py:24
  348.7 2.8 collective-permute-start.12
  350.0 5.6 collective-permute-start.13
  355.7 7.6 %collective-permute-start.14 = (f32[4,56,4]{2,1,0:T(8,128)S(1)}, f32[4,56,4]{2,1,0:T(8,128)S(1)}, u32[]{:S(2)}, u32[]{:S(2)}) collective-permute-start(f32[4,56,4]{2,1,0:T(8,128)S(1)} %get-tuple-element.309), channel_id=1, source_target_pairs={{0,1},{1,2},{2,3},{3,4},{4,5},{5,6},{6,7},{8,9},{9,10},{10,11},{11... | collective-permute-start | bytes 10760 | tf_op jit(solution)/shard_map/ppermute | solution.py:23
  358.0 9.0 %collective-permute-start.15 = (f32[4,56,4]{2,1,0:T(8,128)S(1)}, f32[4,56,4]{2,1,0:T(8,128)S(1)}, u32[]{:S(2)}, u32[]{:S(2)}) collective-permute-start(f32[4,56,4]{2,1,0:T(8,128)S(1)} %get-tuple-element.310), channel_id=1, source_target_pairs={{1,0},{2,1},{3,2},{4,3},{5,4},{6,5},{7,6},{9,8},{10,9},{11,10},{12... | collective-permute-start | bytes 10760 | tf_op jit(solution)/shard_map/ppermute | solution.py:24
  479.0 10.5 %collective-permute-start.17 = (f32[40,4,128]{2,0,1:T(8,128)}, f32[40,4,128]{2,0,1:T(8,128)}, u32[]{:S(2)}, u32[]{:S(2)}) collective-permute-start(f32[40,4,128]{2,0,1:T(8,128)} %copy.100), channel_id=1, source_target_pairs={{8,0},{16,8},{24,16},{9,1},{17,9},{25,17},{10,2},{18,10},{26,18},{... | collective-permute-start | bytes 245768 | tf_op jit(solution)/shard_map/ppermute | solution.py:24
  480.3 6.0 collective-permute-start.16
  494.0 8.6 %collective-permute-start.18 = (f32[40,56,4]{1,0,2:T(8,128)S(1)}, f32[40,56,4]{1,0,2:T(8,128)S(1)}, u32[]{:S(2)}, u32[]{:S(2)}) collective-permute-start(f32[40,56,4]{1,0,2:T(8,128)S(1)} %get-tuple-element.290), channel_id=1, source_target_pairs={{0,1},{1,2},{2,3},{3,4},{4,5},{5,6},{6,7},{8,9},{9,10},{10,11},{11... | collective-permute-start | bytes 107528 | tf_op jit(solution)/shard_map/ppermute | solution.py:23
  498.5 6.3 collective-permute-start.19
  (22 other events, 379.1 us)
Sparse Core Ops, SparseCore 0:
  571.6 127.7 all-reduce.3
